TPU v7x, 32 devices: a whole 2x2x4 slice. The times are simulated.
32 devices in a mesh: path: 16 (over z, x, core), shard: 2 (over y).
Axes of the slice: x: 2, y: 2, z: 4, core: 2. Of those that a mesh axis runs over, the one named last changes fastest.
Arguments:
- deltas: bfloat16 [16, 32, 4096], P('path', 'shard'), may hold values from -96 to 96
- momentum: float32 [16, 32, 4096], P(None, 'shard', 'path'), may hold values from -4 to 4
- path_module: int32 [16], replicated, may hold values from 0 to 15, as said below
Outputs:
- path_update: bfloat16 [16, 32, 4096], P('path', 'shard')
- new_momentum: float32 [16, 32, 4096], P(None, 'shard', 'path')
Inputs may be any that keep to these rules, and one draw needn't show every extreme that they name: `path_module`: every module is used by at least one and at most seven paths.
All inputs are finite; a program needn't handle non-finite values.
Results may differ from a plain program's by a relative error of at most 0.0004.
Values may be sent and summed in bfloat16 or wider, within the bound.
A program may use at most 64 MiB of HBM per device.

v0:
```python
import jax
import jax.numpy as jnp
from jax import lax
from jax.sharding import PartitionSpec as P

D = 4096
outer_rate = 0.7
momentum_rate = 0.9
clip_ratio = 2.0


def local(deltas, momentum, path_module):
    own_index = lax.axis_index("path")
    modules = momentum.shape[0]
    row_count = deltas.shape[1]
    onehot = (path_module[:, None] == jnp.arange(modules, dtype=jnp.int32)[None, :]).astype(
        jnp.float32
    )
    counts = jnp.sum(onehot, axis=0)
    own_module = lax.dynamic_index_in_dim(path_module, own_index, 0, keepdims=False)
    column_pieces = lax.all_to_all(deltas, "path", split_axis=2, concat_axis=0, tiled=True)
    totals = jnp.einsum(
        "pm,prc->mrc",
        onehot.astype(jnp.bfloat16),
        column_pieces,
        preferred_element_type=jnp.float32,
    )
    outer_grad = totals / counts[:, None, None]
    local_squares = jnp.sum(outer_grad * outer_grad, axis=(1, 2))
    norm_squares = lax.psum(local_squares, ("path", "shard"))
    limit = clip_ratio * jnp.sqrt(jnp.float32(row_count * lax.axis_size("shard") * D))
    shrink = jnp.minimum(1.0, limit / jnp.sqrt(norm_squares + 1e-06))
    clipped = outer_grad * shrink[:, None, None]
    new_momentum = momentum_rate * momentum + clipped
    outer_step = (outer_rate * (clipped + momentum_rate * new_momentum)).astype(jnp.bfloat16)
    gathered = lax.all_gather(outer_step, "path", axis=2, tiled=True)
    path_update = lax.dynamic_index_in_dim(gathered, own_module, 0, keepdims=True)
    return (path_update, new_momentum)


def solution(mesh):
    return jax.shard_map(
        local,
        mesh=mesh,
        in_specs=(P("path", "shard", None), P(None, "shard", "path"), P()),
        out_specs=(P("path", "shard", None), P(None, "shard", "path")),
        check_vma=False,
    )
```

profile of v0, /device:TPU:0, one launch (start us, length us, event | category | flops | bytes accessed | tf_op | source)
XLA Modules:
  0.0 145.2 jit_solution(7055501070345371449)
XLA Ops:
  7.2 4.3 %copy.8 = bf16[1,16,4096]{1,0,2:T(2,128)(2,1)S(1)} copy(bf16[1,16,4096]{2,1,0:T(8,128)(2,1)} %param.3) | data formatting | bytes 262144 | tf_op args[0]
  11.5 0.5 broadcast.26
  12.0 0.0 copy-start.1
  12.0 22.4 %reduce = bf16[4096,16]{1,0:T(8,128)(2,1)S(1)} reduce(bf16[4096,1,16]{2,1,0:T(2,128)(2,1)S(1)} %bitcast.25, bf16[]{:T(256)} %broadcast.26), dimensions={1}, to_apply=%bitcast.15.reduce_sub_computation | reduce | bytes 262146
  34.4 1.8 %reshape.8 = bf16[16,2,2048]{2,1,0:T(2,128)(2,1)} reshape(bf16[4096,16]{1,0:T(8,128)(2,1)S(1)} %reduce) | data formatting | bytes 262144
  36.2 7.4 %all-to-all-start = ((bf16[16,2,2048]{2,1,0:T(2,128)(2,1)}), bf16[16,2,2048]{2,1,0:T(2,128)(2,1)S(1)}, u32[]{:S(2)}, u32[]{:S(2)}) async-start(bf16[16,2,2048]{2,1,0:T(2,128)(2,1)} %reshape.8), calls=%async_computation | async-start | bytes 262144 | tf_op jit(solution)/shard_map/all_to_all | solution.py:21
  43.6 0.0 all-gather.2.cloned.1.call-start
  43.6 0.0 copy-done.1
  43.6 0.1 convert_reduce_fusion
  43.8 7.7 %all-to-all-done = bf16[16,2,2048]{2,1,0:T(2,128)(2,1)S(1)} async-done(((bf16[16,2,2048]{2,1,0:T(2,128)(2,1)}), bf16[16,2,2048]{2,1,0:T(2,128)(2,1)S(1)}, u32[]{:S(2)}, u32[]{:S(2)}) %all-to-all-start) | async-done | bytes 131104 | tf_op jit(solution)/shard_map/all_to_all | solution.py:21
  51.5 1.8 %reshape.9 = bf16[4096,1,16]{2,1,0:T(2,128)(2,1)S(1)} reshape(bf16[16,2,2048]{2,1,0:T(2,128)(2,1)S(1)} %all-to-all-done) | data formatting | bytes 262144
  53.3 0.0 copy-start
  53.3 2.0 %copy.9 = bf16[1,16,4096]{2,1,0:T(8,128)(2,1)S(1)} copy(bf16[1,16,4096]{1,0,2:T(2,128)(2,1)S(1)} %bitcast.26) | data formatting | bytes 262144 | tf_op jit(solution)/shard_map/all_to_all | solution.py:21
  55.3 0.3 multiply_reduce_fusion
  55.6 37.5 %psum.7 = f32[16]{0:T(128)S(1)} all-reduce(f32[16]{0:T(128)S(1)} %get-tuple-element.8), channel_id=1, replica_groups=mesh['path'=16,'shard'=2] {'path','shard'}, use_global_device_ids=true, to_apply=%region_2.3 | all-reduce | flops 16 | bytes 128 | tf_op jit(solution)/shard_map/psum | solution.py:30
  93.1 0.0 copy-done
  93.1 0.9 fusion
  94.0 0.0 all-gather.2.cloned.1.call-update
  94.0 0.6 dynamic_slice.8
  96.5 0.9 copy.12
  97.4 38.6 %all-gather.2.cloned.1.call-done = bf16[16,16,4096]{2,0,1:T(8,128)(2,1)} async-done(((bf16[16,16,256]{2,0,1:T(8,128)(2,1)}), bf16[16,16,4096]{2,0,1:T(8,128)(2,1)}) %all-gather.2.cloned.1.call-update) | async-done | bytes 2097168 | tf_op jit(solution)/shard_map/all_gather | solution.py:36
  136.0 1.5 %constant_dynamic-slice_fusion = bf16[1,16,4096]{2,0,1:T(2,128)(2,1)S(1)} fusion(bf16[16,16,4096]{2,0,1:T(8,128)(2,1)} %all-gather.2.cloned.1.call-done, s32[]{:T(128)S(6)} %select_n.9), kind=kLoop, calls=%fused_computation.12 | loop fusion | bytes 262148 | tf_op jit(solution)/shard_map/jit(dynamic_index_in_dim)/dynamic_slice | solution.py:37
  137.5 0.8 copy.11
  (2 shorter events, 0.0 us)
Async XLA Ops:
  12.0 31.6 %copy-start.1 = (s32[16]{0:T(128)S(1)}, s32[16]{0:T(128)}, u32[]{:S(2)}) copy-start(s32[16]{0:T(128)} %param.5) | copy-start | bytes 196
  36.2 15.3 %all-to-all-start = ((bf16[16,2,2048]{2,1,0:T(2,128)(2,1)}), bf16[16,2,2048]{2,1,0:T(2,128)(2,1)S(1)}, u32[]{:S(2)}, u32[]{:S(2)}) async-start(bf16[16,2,2048]{2,1,0:T(2,128)(2,1)} %reshape.8), calls=%async_computation | async-start | bytes 262144 | tf_op jit(solution)/shard_map/all_to_all | solution.py:21
  43.6 92.4 %all-gather.2.cloned.1.call-start = ((), (), s32[]{:S(2)}) async-start(), calls=%async_computation.1 | async-start | bytes 2228224 | tf_op jit(solution)/shard_map/all_gather | solution.py:36
  53.3 39.8 %copy-start = (f32[16,16,256]{2,1,0:T(8,128)S(1)}, f32[16,16,256]{2,1,0:T(8,128)}, u32[]{:S(2)}) copy-start(f32[16,16,256]{2,1,0:T(8,128)} %param.4) | copy-start | bytes 786436
Sparse Core Ops, SparseCore 0:
  94.1 41.7 all-gather.1
where the time goes:
time: 146 us; the launch traced here: 145 us
  waiting for transfers between devices  46.3 us (32%)
  blocking collectives  37.5 us (26%)
  other arithmetic  23.4 us (16%)
  between operations  16 us (11%)
  local copies, waits for them, and re-layouts  14.2 us (10%)
  starting transfers between devices  7.43 us (5%)
    all_gather x1, waiting for transfers between devices, local(): gathered = lax.all_gather(outer_step, 'path', axis=2, tiled=True)  38.6 us
    psum x1, blocking collectives, local(): norm_squares = lax.psum(local_squares, ('path', 'shard'))  37.5 us
    unnamed x1, other arithmetic  22.4 us
    unnamed x11, local copies, waits for them, and re-layouts  10.1 us
    all_to_all x1, waiting for transfers between devices, local(): lax.all_to_all(deltas, 'path', split_axis=2, concat_axis=0, tiled=True)  7.73 us
    all_to_all x1, starting transfers between devices, local(): lax.all_to_all(deltas, 'path', split_axis=2, concat_axis=0, tiled=True)  7.39 us
  transfers between devices with their start and end apart: 2, of which 2 were waited for; matrix products, arithmetic and copies ran while one was open for 1% of the time, Pallas kernels for 0%

commit v1 on v0

--- a/solution.py
+++ b/solution.py
@@ -33,7 +33,10 @@
     clipped = outer_grad * shrink[:, None, None]
     new_momentum = momentum_rate * momentum + clipped
     outer_step = (outer_rate * (clipped + momentum_rate * new_momentum)).astype(jnp.bfloat16)
-    gathered = lax.all_gather(outer_step, "path", axis=2, tiled=True)
+    local_now = jnp.stack([outer_step] * lax.axis_size("path"))
+    gathered = jnp.concatenate(
+        lax.all_to_all(local_now, axis_name="path", split_axis=0, concat_axis=0), axis=2
+    )
     path_update = lax.dynamic_index_in_dim(gathered, own_module, 0, keepdims=True)
     return (path_update, new_momentum)
 

time: 146 us -> 142 us (0.973)
  the two profiles are of different devices: /device:TPU:0 before, /device:TPU:15 now
where the time goes in v1:
time: 142 us; the launch traced here: 141 us
  waiting for transfers between devices  49.1 us (35%)
  blocking collectives  39.3 us (28%)
  other arithmetic  22.8 us (16%)
  local copies, waits for them, and re-layouts  14.4 us (10%)
  starting transfers between devices  12.8 us (9%)
  between operations  2.65 us (2%)
    all_to_all x1, waiting for transfers between devices, local(): lax.all_to_all(local_now, axis_name='path', split_axis=0, concat_axis=0)  44 us
    psum x1, blocking collectives, local(): norm_squares = lax.psum(local_squares, ('path', 'shard'))  39.3 us
    unnamed x1, other arithmetic  22.4 us
    unnamed x10, local copies, waits for them, and re-layouts  9.29 us
    all_to_all x1, starting transfers between devices, local(): lax.all_to_all(deltas, 'path', split_axis=2, concat_axis=0, tiled=True)  6.52 us
    all_to_all x1, starting transfers between devices, local(): lax.all_to_all(local_now, axis_name='path', split_axis=0, concat_axis=0)  6.33 us
    all_to_all x1, waiting for transfers between devices, local(): lax.all_to_all(deltas, 'path', split_axis=2, concat_axis=0, tiled=True)  5.05 us
  transfers between devices with their start and end apart: 2, of which 2 were waited for; matrix products, arithmetic and copies ran while one was open for 1% of the time, Pallas kernels for 0%

profile of v1, /device:TPU:15, one launch (start us, length us, event | category | flops | bytes accessed | tf_op | source)
XLA Modules:
  0.0 141.3 jit_solution(11816285266608062329)
XLA Ops:
  0.6 4.3 %copy.13 = bf16[1,16,4096]{1,0,2:T(2,128)(2,1)S(1)} copy(bf16[1,16,4096]{2,1,0:T(8,128)(2,1)} %param.3) | data formatting | bytes 262144 | tf_op args[0]
  5.0 0.5 broadcast.28
  5.5 0.0 copy-start.1
  5.5 22.4 %reduce = bf16[4096,16]{1,0:T(8,128)(2,1)S(1)} reduce(bf16[4096,1,16]{2,1,0:T(2,128)(2,1)S(1)} %bitcast.29, bf16[]{:T(256)} %broadcast.28), dimensions={1}, to_apply=%bitcast.18.reduce_sub_computation | reduce | bytes 262146
  27.9 1.8 %reshape.18 = bf16[16,2,2048]{2,1,0:T(2,128)(2,1)} reshape(bf16[4096,16]{1,0:T(8,128)(2,1)S(1)} %reduce) | data formatting | bytes 262144
  29.7 6.5 %all-to-all-start = ((bf16[16,2,2048]{2,1,0:T(2,128)(2,1)}), bf16[16,2,2048]{2,1,0:T(2,128)(2,1)S(1)}, u32[]{:S(2)}, u32[]{:S(2)}) async-start(bf16[16,2,2048]{2,1,0:T(2,128)(2,1)} %reshape.18), calls=%async_computation | async-start | bytes 262144 | tf_op jit(solution)/shard_map/all_to_all | solution.py:21
  36.2 0.0 copy-done.1
  36.2 0.1 convert_reduce_fusion
  36.3 5.0 %all-to-all-done = bf16[16,2,2048]{2,1,0:T(2,128)(2,1)S(1)} async-done(((bf16[16,2,2048]{2,1,0:T(2,128)(2,1)}), bf16[16,2,2048]{2,1,0:T(2,128)(2,1)S(1)}, u32[]{:S(2)}, u32[]{:S(2)}) %all-to-all-start) | async-done | bytes 131104 | tf_op jit(solution)/shard_map/all_to_all | solution.py:21
  41.3 1.8 %reshape.19 = bf16[4096,1,16]{2,1,0:T(2,128)(2,1)S(1)} reshape(bf16[16,2,2048]{2,1,0:T(2,128)(2,1)S(1)} %all-to-all-done) | data formatting | bytes 262144
  43.2 0.0 copy-start
  43.2 2.0 %copy.14 = bf16[1,16,4096]{2,1,0:T(8,128)(2,1)S(1)} copy(bf16[1,16,4096]{1,0,2:T(2,128)(2,1)S(1)} %bitcast.30) | data formatting | bytes 262144 | tf_op jit(solution)/shard_map/all_to_all | solution.py:21
  45.2 0.3 multiply_reduce_fusion
  45.5 39.3 %psum.7 = f32[16]{0:T(128)S(1)} all-reduce(f32[16]{0:T(128)S(1)} %get-tuple-element.10), channel_id=1, replica_groups=mesh['path'=16,'shard'=2] {'path','shard'}, use_global_device_ids=true, to_apply=%region_2.3 | all-reduce | flops 16 | bytes 128 | tf_op jit(solution)/shard_map/psum | solution.py:30
  84.8 0.0 copy-done
  84.8 0.2 fusion
  85.1 1.6 %stack.2 = bf16[16,16,16,256]{3,2,1,0:T(8,128)(2,1)} broadcast(bf16[16,16,256]{2,1,0:T(8,128)(2,1)S(1)} %copy.16), dimensions={1,2,3} | broadcast | bytes 2228224 | tf_op jit(solution)/shard_map/stack | solution.py:36
  86.6 6.3 %all-to-all-start.1 = ((bf16[16,16,16,256]{3,2,1,0:T(8,128)(2,1)}), bf16[16,16,16,256]{3,2,1,0:T(8,128)(2,1)S(1)}, u32[]{:S(2)}, u32[]{:S(2)}) async-start(bf16[16,16,16,256]{3,2,1,0:T(8,128)(2,1)} %stack.2), calls=%async_computation.1 | async-start | bytes 4194304 | tf_op jit(solution)/shard_map/all_to_all | solution.py:38
  92.9 0.6 dynamic_slice.8
  95.5 0.9 copy.18
  96.3 44.0 %all-to-all-done.1 = bf16[16,16,16,256]{3,2,1,0:T(8,128)(2,1)S(1)} async-done(((bf16[16,16,16,256]{3,2,1,0:T(8,128)(2,1)}), bf16[16,16,16,256]{3,2,1,0:T(8,128)(2,1)S(1)}, u32[]{:S(2)}, u32[]{:S(2)}) %all-to-all-start.1) | async-done | bytes 2097184 | tf_op jit(solution)/shard_map/all_to_all | solution.py:38
  140.4 0.2 copy.19
  140.6 0.7 constant_dynamic-slice_fusion
  (3 shorter events, 0.1 us)
Async XLA Ops:
  5.5 30.7 %copy-start.1 = (s32[16]{0:T(128)S(1)}, s32[16]{0:T(128)}, u32[]{:S(2)}) copy-start(s32[16]{0:T(128)} %param.5) | copy-start | bytes 196
  29.7 11.7 %all-to-all-start = ((bf16[16,2,2048]{2,1,0:T(2,128)(2,1)}), bf16[16,2,2048]{2,1,0:T(2,128)(2,1)S(1)}, u32[]{:S(2)}, u32[]{:S(2)}) async-start(bf16[16,2,2048]{2,1,0:T(2,128)(2,1)} %reshape.18), calls=%async_computation | async-start | bytes 262144 | tf_op jit(solution)/shard_map/all_to_all | solution.py:21
  43.2 41.6 %copy-start = (f32[16,16,256]{2,1,0:T(8,128)S(1)}, f32[16,16,256]{2,1,0:T(8,128)}, u32[]{:S(2)}) copy-start(f32[16,16,256]{2,1,0:T(8,128)} %param.4) | copy-start | bytes 786436
  86.6 53.7 %all-to-all-start.1 = ((bf16[16,16,16,256]{3,2,1,0:T(8,128)(2,1)}), bf16[16,16,16,256]{3,2,1,0:T(8,128)(2,1)S(1)}, u32[]{:S(2)}, u32[]{:S(2)}) async-start(bf16[16,16,16,256]{3,2,1,0:T(8,128)(2,1)} %stack.2), calls=%async_computation.1 | async-start | bytes 4194304 | tf_op jit(solution)/shard_map/all_to_all | solution.py:38
